TPU v7x, 32 devices: a whole 2x2x4 slice. The times are simulated.
32 devices in a mesh: acq: 8 (over z, y), grp: 4 (over x, core).
Axes of the slice: x: 2, y: 2, z: 4, core: 2. Of those that a mesh axis runs over, the one named last changes fastest.
Arguments:
- tile_slabs: float32 [256, 16, 4096], P(('acq', 'grp')), may hold values from -6 to 6
- dest_rank: int32 [256, 1], replicated, may hold values from 0 to 7; in each aligned block of 8 rows (0 to 7, 8 to 15, ...) at most 2 rows name the same one
- block_slot: int32 [256], replicated, may hold values from 0 to 15
- shifts: float32 [256, 3], replicated, may hold values from 0 to 1
- blend_weight: float32 [256], replicated, may hold values from 0.25 to 4
- parent_map: int32 [512], P(('acq', 'grp')), may hold values from 0 to 63
Outputs:
- pyramid: float32 [64, 8, 8, 1024], P(('acq', 'grp'))
Inputs may be any that keep to these rules, and one draw needn't show every extreme that they name: `dest_rank`: among the rows of one device, no acq index is named more than 2 times, a bound that some block reaches.
All inputs are finite; a program needn't handle non-finite values.
Results may differ from a plain program's by a relative error of at most 0.0003.
Values sent between devices are 32-bit elements; how exact they have to be, the bound alone decides.
A program may use at most 256 MiB of HBM per device.

v0:
```python
import functools
import jax
import jax.numpy as jnp
from jax import lax
from jax.experimental import pallas as pl
from jax.experimental.pallas import tpu as pltpu
from jax.sharding import PartitionSpec as P

BZ = 16
BY = 32
BX = 128
PAR_DEV = 2
HZ, HY, HX = BZ // 2, BY // 2, BX // 2
PAIRS = HY // 2
LANES = HY * HX
VMEM_LIMIT = 62
MESH = pl.DeviceIdType.MESH


def flip(index, mask, count):
    if count & (count - 1):
        return (2 * count + mask - index) % count
    out, bit = index, 1
    while bit < count:
        if mask & bit:
            out = out + bit * (1 - 2 * ((index // bit) % 2))
        bit *= 2
    return out


def partners(count):
    return list(range(1, count)) if count & (count - 1) == 0 else list(range(count))


def halving_matrix():
    row = lax.broadcasted_iota(jnp.int32, (2 * BX, 2 * BX), 0)
    col = lax.broadcasted_iota(jnp.int32, (2 * BX, 2 * BX), 1)
    x, y = row % BX, row // BX
    cx, cy, part = col % HX, (col // HX) % 2, col // BX
    same = y == cy
    both = jnp.where(same & (x // 2 == cx), 1.0, 0.0)
    ahead = jnp.where(same & (x == jnp.minimum(2 * cx + 2, BX - 1)), 1.0, 0.0)
    here = jnp.where(same & (x == 2 * cx), 1.0, 0.0)
    return jnp.where(part == 0, both, ahead - here).astype(jnp.bfloat16)


def split(values):
    high = values.astype(jnp.bfloat16)
    return high, (values - high.astype(jnp.float32)).astype(jnp.bfloat16)


def kernel(
    n_acq, n_grp, cap, tile_hbm, dest_hbm, slot_hbm, weight_hbm, shift_hbm, parent_hbm, out,
    dest, slot, weight, shift, parent, dest_row, slot_row, weight_row,
    tile, thin, high, low, half, factor, send, gath, named,
    meta_sem, load_sem, send_a, recv_a, send_x, recv_x, send_c, recv_c, send_p, recv_p,
):
    count = tile.shape[0]
    a, g = lax.axis_index("acq"), lax.axis_index("grp")
    hi, lo = g // 2, g % 2
    mate = hi * 2 + (1 - lo)
    n_hi = n_grp // 2
    rows = PAIRS * HZ

    barrier = pltpu.get_barrier_semaphore()
    for d in range(1, n_acq):
        pl.semaphore_signal(barrier, inc=1, device_id=((a + d) % n_acq, g), device_id_type=MESH)
    for d in range(1, n_grp):
        pl.semaphore_signal(barrier, inc=1, device_id=(a, (g + d) % n_grp), device_id_type=MESH)

    metas = [
        pltpu.make_async_copy(start, end, meta_sem.at[i])
        for i, (start, end) in enumerate((
            (dest_hbm, dest), (slot_hbm, slot), (weight_hbm, weight), (shift_hbm, shift),
            (parent_hbm, parent), (dest_hbm, dest_row), (slot_hbm, slot_row), (weight_hbm, weight_row),
        ))
    ]
    for meta in metas:
        meta.start()
    loads = [pltpu.make_async_copy(tile_hbm.at[s], tile.at[s], load_sem.at[s]) for s in range(count)]
    for load in loads:
        load.start()

    matrix = halving_matrix()
    last = lax.broadcasted_iota(jnp.int32, (HZ, BX), 0) == HZ - 1
    for meta in metas:
        meta.wait()

    blocks = parent.shape[1]
    base = (a * n_grp + g) * count
    target = [dest[0, base + s] for s in range(count)]
    key = [target[s] * blocks + slot[0, base + s] for s in range(count)]
    subs = lax.broadcasted_iota(jnp.int32, dest_row.shape, 1)
    keys = jnp.where(
        (subs // count) % n_grp == g, dest_row[...] * blocks + slot_row[...], -1
    )
    for s in range(count):
        denom = jnp.sum(jnp.where(keys == key[s], weight_row[...], 0.0), axis=1, keepdims=True)
        factor[s] = jnp.broadcast_to(
            (0.125 * weight[0, base + s]) / jnp.maximum(denom, 1.0), (HZ, BX)
        )
    factor[count] = jnp.zeros((HZ, BX), jnp.float32)
    spot = []
    for s in range(count):
        at = target[s] * cap
        for before in range(s):
            at = at + jnp.where(target[before] == target[s], 1, 0)
        spot.append(at)

    def soften(s, carry):
        pltpu.make_async_copy(tile_hbm.at[s], tile.at[s], load_sem.at[s]).wait()
        fz, fy = shift[0, base + s], shift[1, base + s]

        def row(y):
            return tile[s, :, pl.ds(y * BX, BX)]

        here = row(0)
        for j in range(HY):
            odd = row(2 * j + 1)
            ahead = row(2 * j + 2) if j < HY - 1 else odd
            thin[s, j] = here + odd + fy * (ahead - here)
            here = ahead
        for j in range(HY):
            even = thin[s, j, pl.ds(0, HZ, stride=2), :]
            odd = thin[s, j, pl.ds(1, HZ, stride=2), :]
            ahead = jnp.where(last, odd, pltpu.roll(even, HZ - 1, 0))
            top, rest = split(even + odd + fz * (ahead - even))
            place = (pl.ds((j // 2) * HZ, HZ), pl.ds((j % 2) * BX, BX))
            high[s, place[0], place[1]] = top.astype(jnp.float32)
            low[s, place[0], place[1]] = rest.astype(jnp.float32)
        return carry

    lax.fori_loop(0, count, soften, 0)

    def halve(s, carry):
        half[s] = jnp.dot(
            high[s].astype(jnp.bfloat16), matrix, preferred_element_type=jnp.float32
        ) + jnp.dot(low[s].astype(jnp.bfloat16), matrix, preferred_element_type=jnp.float32)
        return carry

    lax.fori_loop(0, count, halve, 0, unroll=True)
    half[count] = jnp.zeros((rows, 2 * BX), jnp.float32)

    for place in range(n_acq * cap):
        s = count
        for i in range(count):
            s = jnp.where(spot[i] == place, i, s)
        fx = shift[2, base + jnp.minimum(s, count - 1)]
        value = half[s, :, pl.ds(0, BX)] + fx * half[s, :, pl.ds(BX, BX)]
        scale = factor[s]
        for p in range(PAIRS):
            send[place // cap, pl.ds((place % cap) * HZ, HZ), pl.ds(p * BX, BX)] = scale * value[
                p * HZ : (p + 1) * HZ
            ]

    pl.semaphore_wait(barrier, n_acq - 1 + n_grp - 1)

    def to_acq(peer):
        return pltpu.make_async_remote_copy(
            src_ref=send.at[peer], dst_ref=gath.at[g, a],
            send_sem=send_a.at[peer], recv_sem=recv_a.at[a],
            device_id=(peer, g), device_id_type=MESH,
        )

    def from_acq(peer):
        return pltpu.make_async_remote_copy(
            src_ref=send.at[peer], dst_ref=gath.at[g, peer],
            send_sem=send_a.at[peer], recv_sem=recv_a.at[peer],
            device_id=(peer, g), device_id_type=MESH,
        )

    def across(owner, part, peer, sends, recvs, at):
        first, size = parts[part][1:]
        rows_ref = gath.at[owner, pl.ds(first, size)]
        return pltpu.make_async_remote_copy(
            src_ref=rows_ref, dst_ref=rows_ref,
            send_sem=sends.at[at, part], recv_sem=recvs.at[owner, part],
            device_id=(a, peer), device_id_type=MESH,
        )

    gath[g, a] = send[a]
    order = [flip(a, d, n_acq) for d in partners(n_acq)]
    for peer in order:
        to_acq(peer).start()

    steps = [a] + order
    parts = []
    for i, k in enumerate(steps):
        if i < 2 or n_acq & (n_acq - 1):
            parts.append(([i], k, 1))
        elif i % 2 == 1:
            parts.append(([i - 1, i], (k // 2) * 2, 2))

    others = [((hi + d) % n_hi) * 2 + lo for d in range(1, n_hi)]
    origins = [((hi + n_hi - d) % n_hi) * 2 + lo for d in range(1, n_hi)]
    mates = [mate] + [((hi + n_hi - d) % n_hi) * 2 + 1 - lo for d in range(1, n_hi)]

    def forward(k):
        for d, peer in enumerate(others):
            across(g, k, peer, send_x, recv_x, d).start()
        across(g, k, mate, send_c, recv_c, 0).start()

    def relay(k):
        for d, owner in enumerate(origins):
            across(owner, k, mate, send_x, recv_x, d).wait_recv()
            across(owner, k, mate, send_c, recv_c, d + 1).start()

    depth = n_acq * cap * HZ
    tall = PAR_DEV * 8 * HZ
    lane = lax.broadcasted_iota(jnp.int32, (HZ, depth), 1)

    def name(k, found):
        first = (k * n_grp + g) * count
        seen = 0
        slots = [0] * cap
        for s in range(count):
            hit = jnp.where(dest[0, first + s] == a, 1, 0)
            for c in range(cap):
                slots[c] = jnp.where(
                    (hit == 1) & (seen == c), slot[0, first + s], slots[c]
                )
            seen = seen + hit
        for c in range(cap):
            found = jnp.where(lane // HZ == k * cap + c, parent[0, slots[c]], found)
        return found

    forward(0)
    named[g] = lax.fori_loop(0, n_acq, name, jnp.zeros((HZ, depth), jnp.int32))

    def telling(d, owner, peer):
        return pltpu.make_async_remote_copy(
            src_ref=named.at[owner], dst_ref=named.at[owner],
            send_sem=send_p.at[d], recv_sem=recv_p.at[owner],
            device_id=(a, peer), device_id_type=MESH,
        )

    for d in range(1, n_grp):
        telling(d, g, (g + d) % n_grp).start()

    upright = lax.broadcasted_iota(jnp.int32, (tall, depth), 0) + g * tall
    across_lane = lax.broadcasted_iota(jnp.int32, (tall, depth), 1) % HZ

    def place_rows(owner):
        placing = jnp.where(
            named[owner, pl.ds(0, 1), :] * HZ + across_lane == upright, 1.0, 0.0
        ).astype(jnp.bfloat16)
        top, rest = split(gath[owner].reshape(depth, LANES))
        return jnp.dot(placing, top, preferred_element_type=jnp.float32) + jnp.dot(
            placing, rest, preferred_element_type=jnp.float32
        )

    for part in range(1, len(parts)):
        for i in parts[part][0]:
            from_acq(steps[i]).wait_recv()
        forward(part)
        relay(part - 1)
    out[...] = place_rows(g)
    for d in range(1, n_grp):
        owner = (g + n_grp - d) % n_grp
        telling(d, owner, owner).wait_recv()
    for k in range(len(parts)):
        across(mate, k, mate, send_c, recv_c, 0).wait_recv()
    out[...] += place_rows(mate)
    relay(len(parts) - 1)
    for owner in origins:
        out[...] += place_rows(owner)
    for owner in mates[1:]:
        for k in range(len(parts)):
            across(owner, k, mate, send_c, recv_c, 0).wait_recv()
        out[...] += place_rows(owner)

    for peer in order:
        to_acq(peer).wait_send()
    for d in range(1, n_grp):
        telling(d, g, (g + d) % n_grp).wait_send()
    for k in range(len(parts)):
        for d, peer in enumerate(others):
            across(g, k, peer, send_x, recv_x, d).wait_send()
        across(g, k, mate, send_c, recv_c, 0).wait_send()
        for d, owner in enumerate(origins):
            across(owner, k, mate, send_c, recv_c, d + 1).wait_send()


def body(tile_slabs, dest_rank, block_slot, shifts, blend_weight, parent_map):
    n_acq, n_grp = lax.axis_size("acq"), lax.axis_size("grp")
    count = tile_slabs.shape[0]
    subs = dest_rank.shape[0]
    blocks = parent_map.shape[0]
    cap = max(2, 2 * count // n_acq)
    depth = n_acq * cap * HZ
    hbm = pl.BlockSpec(memory_space=pltpu.HBM)
    rows = PAIRS * HZ
    dma = pltpu.SemaphoreType.DMA
    n_hi = n_grp // 2
    summed = pl.pallas_call(
        functools.partial(kernel, n_acq, n_grp, cap),
        out_shape=jax.ShapeDtypeStruct((PAR_DEV * 8 * HZ, LANES), jnp.float32),
        in_specs=[hbm] * 6,
        out_specs=pl.BlockSpec(memory_space=pltpu.VMEM),
        scratch_shapes=[
            pltpu.SMEM((1, subs), jnp.int32),
            pltpu.SMEM((1, subs), jnp.int32),
            pltpu.SMEM((1, subs), jnp.float32),
            pltpu.SMEM((3, subs), jnp.float32),
            pltpu.SMEM((1, blocks), jnp.int32),
            pltpu.VMEM((1, subs), jnp.int32),
            pltpu.VMEM((1, subs), jnp.int32),
            pltpu.VMEM((1, subs), jnp.float32),
            pltpu.VMEM((count, BZ, BY * BX), jnp.float32),
            pltpu.VMEM((count, HY, BZ, BX), jnp.float32),
            pltpu.VMEM((count, rows, 2 * BX), jnp.float32),
            pltpu.VMEM((count, rows, 2 * BX), jnp.float32),
            pltpu.VMEM((count + 1, rows, 2 * BX), jnp.float32),
            pltpu.VMEM((count + 1, HZ, BX), jnp.float32),
            pltpu.VMEM((n_acq, cap * HZ, LANES), jnp.float32),
            pltpu.VMEM((n_grp, n_acq, cap * HZ, LANES), jnp.float32),
            pltpu.VMEM((n_grp, HZ, depth), jnp.int32),
            dma((8,)), dma((count,)),
            dma((n_acq,)), dma((n_acq,)),
            dma((max(1, n_hi - 1), n_acq)), dma((n_grp, n_acq)),
            dma((n_hi, n_acq)), dma((n_grp, n_acq)),
            dma((n_grp,)), dma((n_grp,)),
        ],
        compiler_params=pltpu.CompilerParams(
            collective_id=0, has_side_effects=True, vmem_limit_bytes=VMEM_LIMIT * 2**20
        ),
    )(
        tile_slabs, dest_rank.reshape(1, subs), block_slot.reshape(1, subs),
        blend_weight.reshape(1, subs), shifts.T, parent_map.reshape(1, blocks),
    )
    return summed.reshape(PAR_DEV, 8, HZ, LANES)


def solution(mesh):
    placed = (P(("acq", "grp"), None, None), P(), P(), P(), P(), P(("acq", "grp")))
    return jax.shard_map(
        body,
        mesh=mesh,
        in_specs=placed,
        out_specs=P(("acq", "grp"), None, None, None),
        check_vma=False,
    )
```

profile of v0, /device:TPU:5, one launch (start us, length us, event | category | flops | bytes accessed | tf_op | source)
XLA Modules:
  0.0 27.4 jit_solution(7842429323192950724)
XLA Ops:
  0.0 25.5 %shard_map.64 = f32[128,1024]{1,0:T(8,128)} custom-call(f32[8,16,4096]{2,1,0:T(8,128)} %tile_hbm.1, s32[1,256]{1,0:T(1,128)} %bitcast.8, s32[1,256]{1,0:T(1,128)} %bitcast.9, f32[1,256]{1,0:T(1,128)} %bitcast.10, f32[3,256]{1,0:T(4,128)} %bitcast.7, s32[1,16]{1,0:T(1,128)} %bitcast.11), custom_call_target="tpu_custom_call" | custom-call | tf_op jit(solution)/shard_map/pallas_call | solution.py:295
  25.5 1.9 %copy.8 = f32[2,8,8,1024]{3,2,1,0:T(8,128)} copy(f32[2,8,8,1024]{3,2,1,0:T(8,128)} %bitcast.6) | data formatting | bytes 1048576
where the time goes:
time: 27.6 us; the launch traced here: 27.4 us
  Pallas kernels  25.5 us (92%)
  local copies, waits for them, and re-layouts  1.89 us (7%)
    pallas_call x1, Pallas kernels, body(): pl.pallas_call(functools.partial(kernel, n_acq, n_grp, cap), out_shape=ja...  25.5 us
    unnamed x1, local copies, waits for them, and re-layouts  1.89 us

commit v1 on v0

--- a/solution.py
+++ b/solution.py
@@ -294,7 +294,7 @@
     n_hi = n_grp // 2
     summed = pl.pallas_call(
         functools.partial(kernel, n_acq, n_grp, cap),
-        out_shape=jax.ShapeDtypeStruct((PAR_DEV * 8 * HZ, LANES), jnp.float32),
+        out_shape=pltpu.VMEM((PAR_DEV * 8 * HZ, LANES), jnp.float32),
         in_specs=[hbm] * 6,
         out_specs=pl.BlockSpec(memory_space=pltpu.VMEM),
         scratch_shapes=[

time: 27.6 us -> 25.7 us (0.931)
  local copies, waits for them, and re-layouts: 1.89 us -> 0.8 us
  Pallas kernels: 25.5 us -> 24.7 us
    unnamed x1, local copies, waits for them, and re-layouts: 1.89 us -> 0.8 us
    pallas_call x1, Pallas kernels: 25.5 us -> 24.7 us  [body(): pl.pallas_call(functools.partial(kernel, n_acq, n_grp, cap), out_shape=pl...]
where the time goes in v1:
time: 25.7 us; the launch traced here: 25.6 us
  Pallas kernels  24.7 us (96%)
  local copies, waits for them, and re-layouts  0.8 us (3%)
    pallas_call x1, Pallas kernels, body(): pl.pallas_call(functools.partial(kernel, n_acq, n_grp, cap), out_shape=pl...  24.7 us
    unnamed x1, local copies, waits for them, and re-layouts  0.8 us

profile of v1, /device:TPU:5, one launch (start us, length us, event | category | flops | bytes accessed | tf_op | source)
XLA Modules:
  0.0 25.6 jit_solution(12286449614367918146)
XLA Ops:
  0.0 24.7 %shard_map.64 = f32[128,1024]{1,0:T(8,128)S(1)} custom-call(f32[8,16,4096]{2,1,0:T(8,128)} %tile_hbm.1, s32[1,256]{1,0:T(1,128)} %bitcast.8, s32[1,256]{1,0:T(1,128)} %bitcast.9, f32[1,256]{1,0:T(1,128)} %bitcast.10, f32[3,256]{1,0:T(4,128)} %bitcast.7, s32[1,16]{1,0:T(1,128)} %bitcast.11), custom_call_target="tpu_custom_call" | custom-call | tf_op jit(solution)/shard_map/pallas_call | solution.py:295
  24.8 0.8 %copy.8 = f32[2,8,8,1024]{3,2,1,0:T(8,128)} copy(f32[2,8,8,1024]{3,2,1,0:T(8,128)S(1)} %bitcast.6) | data formatting | bytes 1048576

commit v2 on v1

--- a/solution.py
+++ b/solution.py
@@ -17,19 +17,58 @@
 MESH = pl.DeviceIdType.MESH
 
 
-def flip(index, mask, count):
-    if count & (count - 1):
-        return (2 * count + mask - index) % count
+def flip(index, mask):
     out, bit = index, 1
-    while bit < count:
-        if mask & bit:
-            out = out + bit * (1 - 2 * ((index // bit) % 2))
+    while bit < 64:
+        out = out + bit * ((mask // bit) % 2) * (1 - 2 * ((index // bit) % 2))
         bit *= 2
     return out
 
 
-def partners(count):
-    return list(range(1, count)) if count & (count - 1) == 0 else list(range(count))
+def orders(count):
+    unit = count // 4
+    if unit < 1:
+        plain = list(range(1, count))
+        return [plain] * 2, [[0] + plain] * 4
+    half = unit - unit // 2
+    side, near, far, farther = [list(range(q * unit, (q + 1) * unit)) for q in range(4)]
+    side = side[1:]
+    sends = [side + near + farther + far, side + near + far + farther]
+    arrivals = [
+        [0] + far[:half] + side + near[:half] + farther + far[half:] + near[half:],
+        [0] + side + near + far + farther,
+        [0] + far[:half] + side + far[half:]
+        + farther[:half] + near[:half] + farther[half:] + near[half:],
+        [0] + side + near + farther[:half] + far + farther[half:],
+    ]
+    return sends, arrivals
+
+
+def layout(index, lo, count):
+    sends, arrivals = orders(count)
+    unit = max(1, count // 4)
+    row = index // unit
+    inner = (row + row // 2) % 2 if count >= 4 else 0
+
+    def pick(*cases):
+        if len(cases) == 2:
+            return cases[0] + inner * (cases[1] - cases[0])
+        below, above = pick(*cases[:2]), pick(*cases[2:])
+        return below + lo * (above - below)
+
+    def landing(d, within, low):
+        if (d // unit) % 4 in (1, 2):
+            within = 1 - within
+        return arrivals[2 * low + within].index(d)
+
+    targets = [
+        (
+            pick(*pair),
+            pick(*[landing(pair[within], within, low) for low in range(2) for within in range(2)]),
+        )
+        for pair in zip(*sends)
+    ]
+    return targets, [pick(*cases) for cases in zip(*arrivals)]
 
 
 def halving_matrix():
@@ -149,68 +188,79 @@
         value = half[s, :, pl.ds(0, BX)] + fx * half[s, :, pl.ds(BX, BX)]
         scale = factor[s]
         for p in range(PAIRS):
-            send[place // cap, pl.ds((place % cap) * HZ, HZ), pl.ds(p * BX, BX)] = scale * value[
-                p * HZ : (p + 1) * HZ
-            ]
+            send[place, :, pl.ds(p * BX, BX)] = scale * value[p * HZ : (p + 1) * HZ]
 
     pl.semaphore_wait(barrier, n_acq - 1 + n_grp - 1)
 
-    def to_acq(peer):
+    def to_acq(i, c):
+        d, spot_at = sends[i]
+        peer = flip(a, d)
         return pltpu.make_async_remote_copy(
-            src_ref=send.at[peer], dst_ref=gath.at[g, a],
-            send_sem=send_a.at[peer], recv_sem=recv_a.at[a],
+            src_ref=send.at[peer * cap + c], dst_ref=gath.at[g, spot_at * cap + c],
+            send_sem=send_a.at[0], recv_sem=recv_a.at[spot_at * cap + c],
             device_id=(peer, g), device_id_type=MESH,
         )
 
-    def from_acq(peer):
+    def from_acq(i):
         return pltpu.make_async_remote_copy(
-            src_ref=send.at[peer], dst_ref=gath.at[g, peer],
-            send_sem=send_a.at[peer], recv_sem=recv_a.at[peer],
-            device_id=(peer, g), device_id_type=MESH,
-        )
-
-    def across(owner, part, peer, sends, recvs, at):
-        first, size = parts[part][1:]
-        rows_ref = gath.at[owner, pl.ds(first, size)]
+            src_ref=gath.at[g, i], dst_ref=gath.at[g, i],
+            send_sem=send_a.at[0], recv_sem=recv_a.at[i],
+            device_id=(flip(a, order[i // cap]), g), device_id_type=MESH,
+        )
+
+    def along(owner, pieces, peer, send_sem, recv_sem):
+        piece = gath.at[owner, pieces]
         return pltpu.make_async_remote_copy(
-            src_ref=rows_ref, dst_ref=rows_ref,
-            send_sem=sends.at[at, part], recv_sem=recvs.at[owner, part],
+            src_ref=piece, dst_ref=piece, send_sem=send_sem, recv_sem=recv_sem,
             device_id=(a, peer), device_id_type=MESH,
         )
 
-    gath[g, a] = send[a]
-    order = [flip(a, d, n_acq) for d in partners(n_acq)]
-    for peer in order:
-        to_acq(peer).start()
-
-    steps = [a] + order
-    parts = []
-    for i, k in enumerate(steps):
-        if i < 2 or n_acq & (n_acq - 1):
-            parts.append(([i], k, 1))
-        elif i % 2 == 1:
-            parts.append(([i - 1, i], (k // 2) * 2, 2))
+    def over_x(owner, i, peer, d):
+        return along(owner, i, peer, send_x.at[d - 1], recv_x.at[d - 1, i])
+
+    def to_mate(owner, pieces, d, h):
+        return along(owner, pieces, mate, send_c.at[d], recv_c.at[d, h])
+
+    sends, order = layout(a, lo, n_acq)
+    total = n_acq * cap
+    middle = total // 2
+
+    for c in range(cap):
+        gath[g, c] = send[a * cap + c]
+    for i in range(len(sends)):
+        for c in range(cap):
+            to_acq(i, c).start()
 
     others = [((hi + d) % n_hi) * 2 + lo for d in range(1, n_hi)]
     origins = [((hi + n_hi - d) % n_hi) * 2 + lo for d in range(1, n_hi)]
-    mates = [mate] + [((hi + n_hi - d) % n_hi) * 2 + 1 - lo for d in range(1, n_hi)]
-
-    def forward(k):
-        for d, peer in enumerate(others):
-            across(g, k, peer, send_x, recv_x, d).start()
-        across(g, k, mate, send_c, recv_c, 0).start()
-
-    def relay(k):
-        for d, owner in enumerate(origins):
-            across(owner, k, mate, send_x, recv_x, d).wait_recv()
-            across(owner, k, mate, send_c, recv_c, d + 1).start()
+    mates = [((hi + n_hi - d) % n_hi) * 2 + 1 - lo for d in range(1, n_hi)]
+
+    def forward(i):
+        for d, peer in enumerate(others, 1):
+            over_x(g, i, peer, d).start()
+        to_mate(g, i, 0, i // middle).start()
+
+    def relay(i):
+        for d, owner in enumerate(origins, 1):
+            over_x(owner, i, mate, d).wait_recv()
+            to_mate(owner, i, d, i // middle).start()
+
+    def arrived(d, h):
+        owner = [mate, *mates][d]
+        to_mate(owner, pl.ds(h * middle, middle), d, h).wait_recv()
+
+    for c in range(cap):
+        forward(c)
 
     depth = n_acq * cap * HZ
+    side = depth // 2
     tall = PAR_DEV * 8 * HZ
     lane = lax.broadcasted_iota(jnp.int32, (HZ, depth), 1)
-
-    def name(k, found):
-        first = (k * n_grp + g) * count
+    at_slot = (lane % side) // HZ
+
+    found = [jnp.zeros((HZ, depth), jnp.int32)] * 2
+    for p, d in enumerate(order):
+        first = (flip(a, d) * n_grp + g) * count
         seen = 0
         slots = [0] * cap
         for s in range(count):
@@ -220,17 +270,17 @@
                     (hit == 1) & (seen == c), slot[0, first + s], slots[c]
                 )
             seen = seen + hit
+        h = p // (n_acq // 2)
         for c in range(cap):
-            found = jnp.where(lane // HZ == k * cap + c, parent[0, slots[c]], found)
-        return found
-
-    forward(0)
-    named[g] = lax.fori_loop(0, n_acq, name, jnp.zeros((HZ, depth), jnp.int32))
+            at = p * cap + c - h * (side // HZ)
+            found[h] = jnp.where(at_slot == at, parent[0, slots[c]], found[h])
+    for h in range(2):
+        named[g, h] = found[h]
 
     def telling(d, owner, peer):
         return pltpu.make_async_remote_copy(
             src_ref=named.at[owner], dst_ref=named.at[owner],
-            send_sem=send_p.at[d], recv_sem=recv_p.at[owner],
+            send_sem=send_p.at[0], recv_sem=recv_p.at[owner],
             device_id=(a, peer), device_id_type=MESH,
         )
 
@@ -240,45 +290,82 @@
     upright = lax.broadcasted_iota(jnp.int32, (tall, depth), 0) + g * tall
     across_lane = lax.broadcasted_iota(jnp.int32, (tall, depth), 1) % HZ
 
-    def place_rows(owner):
+    def place_rows(owner, h):
         placing = jnp.where(
-            named[owner, pl.ds(0, 1), :] * HZ + across_lane == upright, 1.0, 0.0
+            named[owner, h, pl.ds(0, 1), :] * HZ + across_lane == upright, 1.0, 0.0
         ).astype(jnp.bfloat16)
-        top, rest = split(gath[owner].reshape(depth, LANES))
-        return jnp.dot(placing, top, preferred_element_type=jnp.float32) + jnp.dot(
-            placing, rest, preferred_element_type=jnp.float32
-        )
-
-    for part in range(1, len(parts)):
-        for i in parts[part][0]:
-            from_acq(steps[i]).wait_recv()
-        forward(part)
-        relay(part - 1)
-    out[...] = place_rows(g)
-    for d in range(1, n_grp):
-        owner = (g + n_grp - d) % n_grp
-        telling(d, owner, owner).wait_recv()
-    for k in range(len(parts)):
-        across(mate, k, mate, send_c, recv_c, 0).wait_recv()
-    out[...] += place_rows(mate)
-    relay(len(parts) - 1)
+        rows = gath[owner, pl.ds(h * (side // HZ), side // HZ)].reshape(side, LANES)
+        return jnp.dot(
+            placing, jnp.concatenate(split(rows), axis=0), preferred_element_type=jnp.float32
+        )
+
+    def mine():
+        out[...] = place_rows(g, 0)
+        for d in range(1, n_grp):
+            owner = (g + n_grp - d) % n_grp
+            telling(d, owner, owner).wait_recv()
+        arrived(0, 0)
+        out[...] += place_rows(mate, 0)
+
+    def theirs():
+        for owner in origins:
+            out[...] += place_rows(owner, 0)
+        for d, owner in enumerate(mates, 1):
+            arrived(d, 0)
+            out[...] += place_rows(owner, 0)
+
+    def receive(start, stop):
+        for i in range(start, stop):
+            from_acq(i).wait_recv()
+            forward(i)
+
+    def pass_on(start, stop):
+        for i in range(start, stop):
+            relay(i)
+
+    quarter = max(1, total // 4)
+    eighth = max(1, total // 8)
+    receive(cap, max(cap, quarter))
+    for i in range(max(cap, quarter), middle):
+        receive(i, i + 1)
+        relay(i - max(cap, quarter))
+    done = middle - max(cap, quarter)
+    pass_on(done, middle - eighth)
+    receive(middle, middle + eighth)
+    mine()
+    receive(middle + eighth, middle + quarter)
+    pass_on(middle - eighth, middle)
+    receive(middle + quarter, total - eighth)
+    pass_on(middle, middle + eighth)
+    receive(total - eighth, total)
+    pass_on(middle + eighth, middle + eighth + 1)
+    theirs()
+    pass_on(middle + eighth + 1, total - 2)
+    out[...] += place_rows(g, 1)
+    pass_on(total - 2, total)
+    arrived(0, 1)
+    out[...] += place_rows(mate, 1)
     for owner in origins:
-        out[...] += place_rows(owner)
-    for owner in mates[1:]:
-        for k in range(len(parts)):
-            across(owner, k, mate, send_c, recv_c, 0).wait_recv()
-        out[...] += place_rows(owner)
-
-    for peer in order:
-        to_acq(peer).wait_send()
-    for d in range(1, n_grp):
-        telling(d, g, (g + d) % n_grp).wait_send()
-    for k in range(len(parts)):
-        for d, peer in enumerate(others):
-            across(g, k, peer, send_x, recv_x, d).wait_send()
-        across(g, k, mate, send_c, recv_c, 0).wait_send()
-        for d, owner in enumerate(origins):
-            across(owner, k, mate, send_c, recv_c, d + 1).wait_send()
+        out[...] += place_rows(owner, 1)
+    for d, owner in enumerate(mates, 1):
+        arrived(d, 1)
+        out[...] += place_rows(owner, 1)
+
+    pltpu.make_async_remote_copy(
+        src_ref=send.at[pl.ds(cap, total - cap)], dst_ref=send.at[pl.ds(cap, total - cap)],
+        send_sem=send_a.at[0], recv_sem=recv_a.at[0],
+        device_id=(flip(a, 1), g), device_id_type=MESH,
+    ).wait_send()
+    pltpu.make_async_remote_copy(
+        src_ref=named.at[pl.ds(1, n_grp - 1)], dst_ref=named.at[pl.ds(1, n_grp - 1)],
+        send_sem=send_p.at[0], recv_sem=recv_p.at[0],
+        device_id=(a, mate), device_id_type=MESH,
+    ).wait_send()
+    whole = pl.ds(0, total)
+    for d in range(1, n_hi):
+        along(g, whole, mate, send_x.at[d - 1], recv_x.at[d - 1, 0]).wait_send()
+    for d in range(n_hi):
+        to_mate(g, whole, d, 0).wait_send()
 
 
 def body(tile_slabs, dest_rank, block_slot, shifts, blend_weight, parent_map):
@@ -292,6 +379,7 @@
     rows = PAIRS * HZ
     dma = pltpu.SemaphoreType.DMA
     n_hi = n_grp // 2
+    pieces = n_acq * cap
     summed = pl.pallas_call(
         functools.partial(kernel, n_acq, n_grp, cap),
         out_shape=pltpu.VMEM((PAR_DEV * 8 * HZ, LANES), jnp.float32),
@@ -312,14 +400,14 @@
             pltpu.VMEM((count, rows, 2 * BX), jnp.float32),
             pltpu.VMEM((count + 1, rows, 2 * BX), jnp.float32),
             pltpu.VMEM((count + 1, HZ, BX), jnp.float32),
-            pltpu.VMEM((n_acq, cap * HZ, LANES), jnp.float32),
-            pltpu.VMEM((n_grp, n_acq, cap * HZ, LANES), jnp.float32),
-            pltpu.VMEM((n_grp, HZ, depth), jnp.int32),
+            pltpu.VMEM((n_acq * cap, HZ, LANES), jnp.float32),
+            pltpu.VMEM((n_grp, n_acq * cap, HZ, LANES), jnp.float32),
+            pltpu.VMEM((n_grp, 2, HZ, depth), jnp.int32),
             dma((8,)), dma((count,)),
-            dma((n_acq,)), dma((n_acq,)),
-            dma((max(1, n_hi - 1), n_acq)), dma((n_grp, n_acq)),
-            dma((n_hi, n_acq)), dma((n_grp, n_acq)),
-            dma((n_grp,)), dma((n_grp,)),
+            dma((1,)), dma((pieces,)),
+            dma((max(1, n_hi - 1),)), dma((max(1, n_hi - 1), pieces)),
+            dma((n_hi,)), dma((n_hi, 2)),
+            dma((1,)), dma((n_grp,)),
         ],
         compiler_params=pltpu.CompilerParams(
             collective_id=0, has_side_effects=True, vmem_limit_bytes=VMEM_LIMIT * 2**20

time: 25.7 us -> 24.7 us (0.961)
  the two profiles are of different devices: /device:TPU:5 before, /device:TPU:0 now
where the time goes in v2:
time: 24.7 us; the launch traced here: 24.5 us
  Pallas kernels  23.7 us (96%)
  local copies, waits for them, and re-layouts  0.8 us (3%)
    pallas_call x1, Pallas kernels, body(): pl.pallas_call(functools.partial(kernel, n_acq, n_grp, cap), out_shape=pl...  23.7 us
    unnamed x1, local copies, waits for them, and re-layouts  0.8 us

profile of v2, /device:TPU:0, one launch (start us, length us, event | category | flops | bytes accessed | tf_op | source)
XLA Modules:
  0.0 24.5 jit_solution(151709025824149480)
XLA Ops:
  0.0 23.7 %shard_map.64 = f32[128,1024]{1,0:T(8,128)S(1)} custom-call(f32[8,16,4096]{2,1,0:T(8,128)} %tile_hbm.1, s32[1,256]{1,0:T(1,128)} %bitcast.8, s32[1,256]{1,0:T(1,128)} %bitcast.9, f32[1,256]{1,0:T(1,128)} %bitcast.10, f32[3,256]{1,0:T(4,128)} %bitcast.7, s32[1,16]{1,0:T(1,128)} %bitcast.11), custom_call_target="tpu_custom_call" | custom-call | tf_op jit(solution)/shard_map/pallas_call | solution.py:383
  23.7 0.8 %copy.8 = f32[2,8,8,1024]{3,2,1,0:T(8,128)} copy(f32[2,8,8,1024]{3,2,1,0:T(8,128)S(1)} %bitcast.6) | data formatting | bytes 1048576

commit v3 on v2

v3 whole, which is shorter than its diff:
```python
import functools
import jax
import jax.numpy as jnp
from jax import lax
from jax.experimental import pallas as pl
from jax.experimental.pallas import tpu as pltpu
from jax.sharding import PartitionSpec as P

BZ = 16
BY = 32
BX = 128
PAR_DEV = 2
HZ, HY, HX = BZ // 2, BY // 2, BX // 2
PAIRS = HY // 2
LANES = HY * HX
PER_LOAD = 2
VMEM_LIMIT = 62
MESH = pl.DeviceIdType.MESH


def flip(index, mask):
    out, bit = index, 1
    while bit < 64:
        out = out + bit * ((mask // bit) % 2) * (1 - 2 * ((index // bit) % 2))
        bit *= 2
    return out


def orders(count):
    unit = count // 4
    if unit < 1:
        plain = list(range(1, count))
        return plain, [[0] + plain] * 4
    half = unit - unit // 2
    side, near, far, farther = [list(range(q * unit, (q + 1) * unit)) for q in range(4)]
    side = side[1:]
    sends = side + near + far + farther
    arrivals = [
        [0] + side + far[:half] + near + farther[:half] + far[half:] + farther[half:],
        [0] + sends,
        [0] + far[:half] + side + far[half:] + near + farther,
        [0] + side + near + farther[:half] + far + farther[half:],
    ]
    return sends, arrivals


def layout(index, lo, count):
    sends, arrivals = orders(count)
    unit = max(1, count // 4)
    row = index // unit
    inner = (row + row // 2) % 2 if count >= 4 else 0

    def pick(*cases):
        if len(cases) == 2:
            return cases[0] + inner * (cases[1] - cases[0])
        below, above = pick(*cases[:2]), pick(*cases[2:])
        return below + lo * (above - below)

    def landing(d, within, low):
        if (d // unit) % 4 in (1, 2):
            within = 1 - within
        return arrivals[2 * low + within].index(d)

    targets = [
        (d, pick(*[landing(d, within, low) for low in range(2) for within in range(2)]))
        for d in sends
    ]
    return targets, [pick(*cases) for cases in zip(*arrivals)]


def halving_matrix():
    row = lax.broadcasted_iota(jnp.int32, (2 * BX, 2 * BX), 0)
    col = lax.broadcasted_iota(jnp.int32, (2 * BX, 2 * BX), 1)
    x, y = row % BX, row // BX
    cx, cy, part = col % HX, (col // HX) % 2, col // BX
    same = y == cy
    both = jnp.where(same & (x // 2 == cx), 1.0, 0.0)
    ahead = jnp.where(same & (x == jnp.minimum(2 * cx + 2, BX - 1)), 1.0, 0.0)
    here = jnp.where(same & (x == 2 * cx), 1.0, 0.0)
    return jnp.where(part == 0, both, ahead - here).astype(jnp.bfloat16)


def split(values):
    high = values.astype(jnp.bfloat16)
    return high, (values - high.astype(jnp.float32)).astype(jnp.bfloat16)


def kernel(
    n_acq, n_grp, cap, tile_hbm, dest_hbm, slot_hbm, weight_hbm, shift_hbm, parent_hbm, out,
    named_by, weight, shift, parent, named_rows, weight_row,
    tile, thin, high, low, half, factor, send, gath, named,
    meta_sem, load_sem, send_a, recv_a, send_x, recv_x, send_c, recv_c, send_p, recv_p,
):
    count = tile.shape[0]
    a, g = lax.axis_index("acq"), lax.axis_index("grp")
    hi, lo = g // 2, g % 2
    mate = hi * 2 + (1 - lo)
    n_hi = n_grp // 2
    rows = PAIRS * HZ

    barrier = pltpu.get_barrier_semaphore()
    for d in range(1, n_acq):
        pl.semaphore_signal(barrier, inc=1, device_id=((a + d) % n_acq, g), device_id_type=MESH)
    for d in range(1, n_grp):
        pl.semaphore_signal(barrier, inc=1, device_id=(a, (g + d) % n_grp), device_id_type=MESH)

    dest, slot = named_by.at[0], named_by.at[1]
    metas = [
        pltpu.make_async_copy(start, end, meta_sem.at[i])
        for start, end, i in (
            (dest_hbm, dest, 0), (slot_hbm, slot, 0), (weight_hbm, weight, 1),
            (shift_hbm, shift, 2), (parent_hbm, parent, 3),
            (dest_hbm, named_rows.at[0], 4), (slot_hbm, named_rows.at[1], 4),
            (weight_hbm, weight_row, 5),
        )
    ]
    for meta in metas:
        meta.start()

    def load(i):
        some = pl.ds(i * PER_LOAD, PER_LOAD)
        return pltpu.make_async_copy(tile_hbm.at[some], tile.at[some], load_sem.at[i])

    for i in range(count // PER_LOAD):
        load(i).start()

    matrix = halving_matrix()
    last = lax.broadcasted_iota(jnp.int32, (HZ, BX), 0) == HZ - 1
    for pair, i in ((named_by, 0), (named_rows, 4)):
        pltpu.make_async_copy(pair, pair, meta_sem.at[i]).wait()
    for i in (2, 3, 4, 7):
        metas[i].wait()

    blocks = parent.shape[1]
    base = (a * n_grp + g) * count
    target = [dest[0, base + s] for s in range(count)]
    key = [target[s] * blocks + slot[0, base + s] for s in range(count)]
    subs = lax.broadcasted_iota(jnp.int32, weight_row.shape, 1)
    keys = jnp.where(
        (subs // count) % n_grp == g, named_rows[0] * blocks + named_rows[1], -1
    )
    for s in range(count):
        denom = jnp.sum(jnp.where(keys == key[s], weight_row[...], 0.0), axis=1, keepdims=True)
        factor[s] = jnp.broadcast_to(
            (0.125 * weight[0, base + s]) / jnp.maximum(denom, 1.0), (HZ, BX)
        )
    factor[count] = jnp.zeros((HZ, BX), jnp.float32)
    spot = []
    for s in range(count):
        at = target[s] * cap
        for before in range(s):
            at = at + jnp.where(target[before] == target[s], 1, 0)
        spot.append(at)

    def soften(s):
        fz, fy = shift[0, base + s], shift[1, base + s]

        def row(y):
            return tile[s, :, pl.ds(y * BX, BX)]

        here = row(0)
        for j in range(HY):
            odd = row(2 * j + 1)
            ahead = row(2 * j + 2) if j < HY - 1 else odd
            thin[s, j] = here + odd + fy * (ahead - here)
            here = ahead
        for j in range(HY):
            even = thin[s, j, pl.ds(0, HZ, stride=2), :]
            odd = thin[s, j, pl.ds(1, HZ, stride=2), :]
            ahead = jnp.where(last, odd, pltpu.roll(even, HZ - 1, 0))
            top, rest = split(even + odd + fz * (ahead - even))
            place = (pl.ds((j // 2) * HZ, HZ), pl.ds((j % 2) * BX, BX))
            high[s, place[0], place[1]] = top.astype(jnp.float32)
            low[s, place[0], place[1]] = rest.astype(jnp.float32)

    def loaded(i, carry):
        load(i).wait()
        for s in range(PER_LOAD):
            soften(i * PER_LOAD + s)
        return carry

    lax.fori_loop(0, count // PER_LOAD, loaded, 0)

    def halve(s, carry):
        half[s] = jnp.dot(
            high[s].astype(jnp.bfloat16), matrix, preferred_element_type=jnp.float32
        ) + jnp.dot(low[s].astype(jnp.bfloat16), matrix, preferred_element_type=jnp.float32)
        return carry

    lax.fori_loop(0, count, halve, 0, unroll=True)
    half[count] = jnp.zeros((rows, 2 * BX), jnp.float32)

    for place in range(n_acq * cap):
        s = count
        for i in range(count):
            s = jnp.where(spot[i] == place, i, s)
        fx = shift[2, base + jnp.minimum(s, count - 1)]
        value = half[s, :, pl.ds(0, BX)] + fx * half[s, :, pl.ds(BX, BX)]
        scale = factor[s]
        for p in range(PAIRS):
            send[place, :, pl.ds(p * BX, BX)] = scale * value[p * HZ : (p + 1) * HZ]

    pl.semaphore_wait(barrier, n_acq - 1 + n_grp - 1)

    targets, order = layout(a, lo, n_acq)
    total = n_acq * cap
    middle = total // 2
    direct = total - cap
    received = [(i, cap) for i in range(cap, middle, cap)] + [(i, 1) for i in range(middle, total)]
    groups, first = [], 0
    while first < total:
        size = max(1, (total - first) // 2)
        groups.append((first, size))
        first += size

    def landed(at, c):
        late = at // (n_acq // 2)
        return recv_a.at[at + late * ((at - n_acq // 2) * (cap - 1) + c)]

    def to_acq(d, at, c):
        peer = flip(a, d)
        return pltpu.make_async_remote_copy(
            src_ref=send.at[peer * cap + c], dst_ref=gath.at[g, at * cap + c],
            send_sem=send_a.at[0], recv_sem=landed(at, c),
            device_id=(peer, g), device_id_type=MESH,
        )

    def from_acq(i, size):
        piece = gath.at[g, pl.ds(i, size)]
        return pltpu.make_async_remote_copy(
            src_ref=piece, dst_ref=piece,
            send_sem=send_a.at[0], recv_sem=landed(i // cap, i % cap),
            device_id=(flip(a, order[i // cap]), g), device_id_type=MESH,
        )

    def along(owner, first, size, peer, send_sem, recv_sem):
        piece = gath.at[owner, pl.ds(first, size)]
        return pltpu.make_async_remote_copy(
            src_ref=piece, dst_ref=piece, send_sem=send_sem, recv_sem=recv_sem,
            device_id=(a, peer), device_id_type=MESH,
        )

    others = [((hi + d) % n_hi) * 2 + lo for d in range(1, n_hi)]
    origins = [((hi + n_hi - d) % n_hi) * 2 + lo for d in range(1, n_hi)]
    mates = [((hi + n_hi - d) % n_hi) * 2 + 1 - lo for d in range(1, n_hi)]

    def over_x(owner, first, size, peer, d):
        k = max(k for k, (start, _) in enumerate(groups) if start <= first)
        return along(owner, first, size, peer, send_x.at[d - 1], recv_x.at[d - 1, k])

    def aside(first, size, peer, d):
        return along(g, first, size, peer, send_x.at[d - 1], recv_c.at[d, 1])

    def to_mate(owner, first, size, d):
        return along(owner, first, size, mate, send_c.at[d], recv_c.at[d, first // middle])

    def forward(i, size):
        for d, peer in enumerate(others, 1):
            over_x(g, i, size, peer, d).start()
            if i >= direct:
                @pl.when(lo == 0)
                def _():
                    aside(i, size, (peer // 2) * 2 + 1, d).start()
        to_mate(g, i, size, 0).start()

    def relay(first, size):
        for d, owner in enumerate(origins, 1):
            over_x(owner, first, size, mate, d).wait_recv()
            if first < direct:
                to_mate(owner, first, size, d).start()
            else:
                @pl.when(lo == 1)
                def _():
                    to_mate(owner, first, size, d).start()

    def arrived(d, h):
        to_mate([mate, *mates][d], h * middle, middle, d).wait_recv()

    for c in range(cap):
        gath[g, c] = send[a * cap + c]
    for d, at in targets:
        for c in range(cap):
            to_acq(d, at, c).start()
    forward(0, cap)

    depth = n_acq * cap * HZ
    side = depth // 2
    tall = PAR_DEV * 8 * HZ
    lane = lax.broadcasted_iota(jnp.int32, (HZ, depth), 1)
    at_slot = (lane % side) // HZ

    found = [jnp.zeros((HZ, depth), jnp.int32)] * 2
    for p, d in enumerate(order):
        first = (flip(a, d) * n_grp + g) * count
        seen = 0
        slots = [0] * cap
        for s in range(count):
            hit = jnp.where(dest[0, first + s] == a, 1, 0)
            for c in range(cap):
                slots[c] = jnp.where(
                    (hit == 1) & (seen == c), slot[0, first + s], slots[c]
                )
            seen = seen + hit
        h = p // (n_acq // 2)
        for c in range(cap):
            at = p * cap + c - h * (side // HZ)
            found[h] = jnp.where(at_slot == at, parent[0, slots[c]], found[h])
    for h in range(2):
        named[0, h] = found[h]

    def telling(d, peer):
        return pltpu.make_async_remote_copy(
            src_ref=named.at[0], dst_ref=named.at[d],
            send_sem=send_p.at[0], recv_sem=recv_p.at[0],
            device_id=(a, peer), device_id_type=MESH,
        )

    for d in range(1, n_grp):
        telling(d, (g + d) % n_grp).start()

    upright = lax.broadcasted_iota(jnp.int32, (tall, depth), 0) + g * tall
    across_lane = lax.broadcasted_iota(jnp.int32, (tall, depth), 1) % HZ

    def place_rows(owner, h):
        placing = jnp.where(
            named[(g + n_grp - owner) % n_grp, h, pl.ds(0, 1), :] * HZ + across_lane == upright, 1.0, 0.0
        ).astype(jnp.bfloat16)
        rows = gath[owner, pl.ds(h * (side // HZ), side // HZ)].reshape(side, LANES)
        return jnp.dot(
            placing, jnp.concatenate(split(rows), axis=0), preferred_element_type=jnp.float32
        )

    for i, size in received:
        from_acq(i, size).wait_recv()
        forward(i, size)
    out[...] = place_rows(g, 0)
    out[...] += place_rows(g, 1)
    relay(*groups[0])
    others_named = named.at[pl.ds(1, n_grp - 1)]
    naming = pltpu.make_async_remote_copy(
        src_ref=others_named, dst_ref=others_named,
        send_sem=send_p.at[0], recv_sem=recv_p.at[0],
        device_id=(a, mate), device_id_type=MESH,
    )
    naming.wait_recv()
    for owner in origins:
        out[...] += place_rows(owner, 0)
    for k in range(1, len(groups)):
        relay(*groups[k])
        if k == 1:
            arrived(0, 0)
            out[...] += place_rows(mate, 0)
    arrived(0, 1)
    out[...] += place_rows(mate, 1)
    for d, owner in enumerate(mates, 1):
        arrived(d, 0)
        out[...] += place_rows(owner, 0)
    for owner in origins:
        out[...] += place_rows(owner, 1)
    for d, owner in enumerate(mates, 1):
        arrived(d, 1)
        out[...] += place_rows(owner, 1)

    naming.wait_send()
    left = send.at[pl.ds(cap, total - cap)]
    pltpu.make_async_remote_copy(
        src_ref=left, dst_ref=left, send_sem=send_a.at[0], recv_sem=recv_a.at[0],
        device_id=(flip(a, 1), g), device_id_type=MESH,
    ).wait_send()
    to_mate(g, 0, total, 0).wait_send()
    for d in range(1, n_hi):
        over_x(g, 0, total, mate, d).wait_send()
        to_mate(g, 0, direct, d).wait_send()

        @pl.when(lo == 0)
        def _():
            aside(direct, total - direct, mate, d).wait_send()

        @pl.when(lo == 1)
        def _():
            to_mate(g, direct, total - direct, d).wait_send()


def body(tile_slabs, dest_rank, block_slot, shifts, blend_weight, parent_map):
    n_acq, n_grp = lax.axis_size("acq"), lax.axis_size("grp")
    count = tile_slabs.shape[0]
    subs = dest_rank.shape[0]
    blocks = parent_map.shape[0]
    cap = max(2, 2 * count // n_acq)
    depth = n_acq * cap * HZ
    hbm = pl.BlockSpec(memory_space=pltpu.HBM)
    rows = PAIRS * HZ
    dma = pltpu.SemaphoreType.DMA
    n_hi = n_grp // 2
    pieces = n_acq * cap
    summed = pl.pallas_call(
        functools.partial(kernel, n_acq, n_grp, cap),
        out_shape=pltpu.VMEM((PAR_DEV * 8 * HZ, LANES), jnp.float32),
        in_specs=[hbm] * 6,
        out_specs=pl.BlockSpec(memory_space=pltpu.VMEM),
        scratch_shapes=[
            pltpu.SMEM((2, 1, subs), jnp.int32),
            pltpu.SMEM((1, subs), jnp.float32),
            pltpu.SMEM((3, subs), jnp.float32),
            pltpu.SMEM((1, blocks), jnp.int32),
            pltpu.VMEM((2, 1, subs), jnp.int32),
            pltpu.VMEM((1, subs), jnp.float32),
            pltpu.VMEM((count, BZ, BY * BX), jnp.float32),
            pltpu.VMEM((count, HY, BZ, BX), jnp.float32),
            pltpu.VMEM((count, rows, 2 * BX), jnp.float32),
            pltpu.VMEM((count, rows, 2 * BX), jnp.float32),
            pltpu.VMEM((count + 1, rows, 2 * BX), jnp.float32),
            pltpu.VMEM((count + 1, HZ, BX), jnp.float32),
            pltpu.VMEM((n_acq * cap, HZ, LANES), jnp.float32),
            pltpu.VMEM((n_grp, n_acq * cap, HZ, LANES), jnp.float32),
            pltpu.VMEM((n_grp, 2, HZ, depth), jnp.int32),
            dma((6,)), dma((count // PER_LOAD,)),
            dma((1,)), dma((n_acq // 2 * (1 + cap),)),
            dma((max(1, n_hi - 1),)), dma((max(1, n_hi - 1), pieces.bit_length())),
            dma((n_hi,)), dma((n_hi, 2)),
            dma((1,)), dma((1,)),
        ],
        compiler_params=pltpu.CompilerParams(
            collective_id=0, has_side_effects=True, vmem_limit_bytes=VMEM_LIMIT * 2**20
        ),
    )(
        tile_slabs, dest_rank.reshape(1, subs), block_slot.reshape(1, subs),
        blend_weight.reshape(1, subs), shifts.T, parent_map.reshape(1, blocks),
    )
    return summed.reshape(PAR_DEV, 8, HZ, LANES)


def solution(mesh):
    placed = (P(("acq", "grp"), None, None), P(), P(), P(), P(), P(("acq", "grp")))
    return jax.shard_map(
        body,
        mesh=mesh,
        in_specs=placed,
        out_specs=P(("acq", "grp"), None, None, None),
        check_vma=False,
    )
```

time: 24.7 us -> 23 us (0.931)
  Pallas kernels: 23.7 us -> 22.1 us
    pallas_call x1, Pallas kernels: 23.7 us -> 22.1 us  [body(): pl.pallas_call(functools.partial(kernel, n_acq, n_grp, cap), out_shape=pl...]
where the time goes in v3:
time: 23 us; the launch traced here: 22.9 us
  Pallas kernels  22.1 us (96%)
  local copies, waits for them, and re-layouts  0.8 us (3%)
    pallas_call x1, Pallas kernels, body(): pl.pallas_call(functools.partial(kernel, n_acq, n_grp, cap), out_shape=pl...  22.1 us
    unnamed x1, local copies, waits for them, and re-layouts  0.8 us

profile of v3, /device:TPU:0, one launch (start us, length us, event | category | flops | bytes accessed | tf_op | source)
XLA Modules:
  0.0 22.9 jit_solution(14894071050264061607)
XLA Ops:
  0.0 22.1 %shard_map.64 = f32[128,1024]{1,0:T(8,128)S(1)} custom-call(f32[8,16,4096]{2,1,0:T(8,128)} %tile_hbm.1, s32[1,256]{1,0:T(1,128)} %bitcast.8, s32[1,256]{1,0:T(1,128)} %bitcast.9, f32[1,256]{1,0:T(1,128)} %bitcast.10, f32[3,256]{1,0:T(4,128)} %bitcast.7, s32[1,16]{1,0:T(1,128)} %bitcast.11), custom_call_target="tpu_custom_call" | custom-call | tf_op jit(solution)/shard_map/pallas_call | solution.py:396
  22.1 0.8 %copy.8 = f32[2,8,8,1024]{3,2,1,0:T(8,128)} copy(f32[2,8,8,1024]{3,2,1,0:T(8,128)S(1)} %bitcast.6) | data formatting | bytes 1048576

commit v4 on v3

--- a/solution.py
+++ b/solution.py
@@ -36,7 +36,7 @@
     side = side[1:]
     sends = side + near + far + farther
     arrivals = [
-        [0] + side + far[:half] + near + farther[:half] + far[half:] + farther[half:],
+        [0] + side + far[:half] + near + far[half:] + farther,
         [0] + sends,
         [0] + far[:half] + side + far[half:] + near + farther,
         [0] + side + near + farther[:half] + far + farther[half:],
@@ -89,7 +89,7 @@
     n_acq, n_grp, cap, tile_hbm, dest_hbm, slot_hbm, weight_hbm, shift_hbm, parent_hbm, out,
     named_by, weight, shift, parent, named_rows, weight_row,
     tile, thin, high, low, half, factor, send, gath, named,
-    meta_sem, load_sem, send_a, recv_a, send_x, recv_x, send_c, recv_c, send_p, recv_p,
+    meta_sem, load_sem, send_a, recv_a, send_x, recv_x, send_c, recv_c, send_p, recv_p, recv_r, recv_s,
 ):
     count = tile.shape[0]
     a, g = lax.axis_index("acq"), lax.axis_index("grp")
@@ -103,6 +103,11 @@
         pl.semaphore_signal(barrier, inc=1, device_id=((a + d) % n_acq, g), device_id_type=MESH)
     for d in range(1, n_grp):
         pl.semaphore_signal(barrier, inc=1, device_id=(a, (g + d) % n_grp), device_id_type=MESH)
+    lent = n_acq // 4 + n_acq // 8
+    for d in range(n_acq - lent, n_acq):
+        @pl.when(lo == 1)
+        def _():
+            pl.semaphore_signal(barrier, inc=1, device_id=(flip(a, d), mate), device_id_type=MESH)
 
     dest, slot = named_by.at[0], named_by.at[1]
     metas = [
@@ -151,6 +156,13 @@
         for before in range(s):
             at = at + jnp.where(target[before] == target[s], 1, 0)
         spot.append(at)
+
+    chosen = []
+    for place in range(n_acq * cap):
+        s = count
+        for i in range(count):
+            s = jnp.where(spot[i] == place, i, s)
+        chosen.append(s)
 
     def soften(s):
         fz, fy = shift[0, base + s], shift[1, base + s]
@@ -173,6 +185,11 @@
             high[s, place[0], place[1]] = top.astype(jnp.float32)
             low[s, place[0], place[1]] = rest.astype(jnp.float32)
 
+    def halve(s):
+        half[s] = jnp.dot(
+            high[s].astype(jnp.bfloat16), matrix, preferred_element_type=jnp.float32
+        ) + jnp.dot(low[s].astype(jnp.bfloat16), matrix, preferred_element_type=jnp.float32)
+
     def loaded(i, carry):
         load(i).wait()
         for s in range(PER_LOAD):
@@ -180,57 +197,61 @@
         return carry
 
     lax.fori_loop(0, count // PER_LOAD, loaded, 0)
-
-    def halve(s, carry):
-        half[s] = jnp.dot(
-            high[s].astype(jnp.bfloat16), matrix, preferred_element_type=jnp.float32
-        ) + jnp.dot(low[s].astype(jnp.bfloat16), matrix, preferred_element_type=jnp.float32)
-        return carry
-
-    lax.fori_loop(0, count, halve, 0, unroll=True)
+    for s in range(count):
+        halve(s)
+
     half[count] = jnp.zeros((rows, 2 * BX), jnp.float32)
 
     for place in range(n_acq * cap):
-        s = count
-        for i in range(count):
-            s = jnp.where(spot[i] == place, i, s)
+        s = chosen[place]
         fx = shift[2, base + jnp.minimum(s, count - 1)]
         value = half[s, :, pl.ds(0, BX)] + fx * half[s, :, pl.ds(BX, BX)]
         scale = factor[s]
         for p in range(PAIRS):
             send[place, :, pl.ds(p * BX, BX)] = scale * value[p * HZ : (p + 1) * HZ]
 
-    pl.semaphore_wait(barrier, n_acq - 1 + n_grp - 1)
+    pl.semaphore_wait(barrier, n_acq - 1 + n_grp - 1 + lent * (1 - lo))
 
     targets, order = layout(a, lo, n_acq)
     total = n_acq * cap
     middle = total // 2
-    direct = total - cap
-    received = [(i, cap) for i in range(cap, middle, cap)] + [(i, 1) for i in range(middle, total)]
-    groups, first = [], 0
+    shared = total - lent * cap
+    received = [(i, cap) for i in range(cap, middle, cap)] + [(i, 1) for i in range(middle, shared)]
+    groups, first = [(0, shared)], shared
     while first < total:
-        size = max(1, (total - first) // 2)
+        size = max(1, total - cap - first)
         groups.append((first, size))
         first += size
+    halved = list(range(shared + (total - shared) // 3, total - cap))
+    borrowed = (
+        list(range(shared, shared + (total - shared) // 3, 2)) + halved
+        + list(range(shared + 1, shared + (total - shared) // 3, 2)) + list(range(total - cap, total))
+    )
 
     def landed(at, c):
         late = at // (n_acq // 2)
-        return recv_a.at[at + late * ((at - n_acq // 2) * (cap - 1) + c)]
+        return at + late * ((at - n_acq // 2) * (cap - 1) + c)
+
+    def lent_at(i):
+        return n_acq // 2 * (1 + cap) + i - shared
 
     def to_acq(d, at, c):
+        sem, core = landed(at, c), g
+        if d >= n_acq - lent:
+            sem = lo * sem + (1 - lo) * lent_at(d * cap + c)
+            core = g + 1 - lo
         peer = flip(a, d)
         return pltpu.make_async_remote_copy(
             src_ref=send.at[peer * cap + c], dst_ref=gath.at[g, at * cap + c],
-            send_sem=send_a.at[0], recv_sem=landed(at, c),
-            device_id=(peer, g), device_id_type=MESH,
-        )
-
-    def from_acq(i, size):
-        piece = gath.at[g, pl.ds(i, size)]
+            send_sem=send_a.at[0], recv_sem=recv_a.at[sem],
+            device_id=(peer, core), device_id_type=MESH,
+        )
+
+    def from_acq(owner, i, size, sem):
+        piece = gath.at[owner, pl.ds(i, size)]
         return pltpu.make_async_remote_copy(
-            src_ref=piece, dst_ref=piece,
-            send_sem=send_a.at[0], recv_sem=landed(i // cap, i % cap),
-            device_id=(flip(a, order[i // cap]), g), device_id_type=MESH,
+            src_ref=piece, dst_ref=piece, send_sem=send_a.at[0], recv_sem=recv_a.at[sem],
+            device_id=(flip(a, 1), g), device_id_type=MESH,
         )
 
     def along(owner, first, size, peer, send_sem, recv_sem):
@@ -248,40 +269,62 @@
         k = max(k for k, (start, _) in enumerate(groups) if start <= first)
         return along(owner, first, size, peer, send_x.at[d - 1], recv_x.at[d - 1, k])
 
-    def aside(first, size, peer, d):
-        return along(g, first, size, peer, send_x.at[d - 1], recv_c.at[d, 1])
-
     def to_mate(owner, first, size, d):
         return along(owner, first, size, mate, send_c.at[d], recv_c.at[d, first // middle])
 
-    def forward(i, size):
+    def take(i, size):
+        from_acq(g, i, size, landed(i // cap, i % cap)).wait_recv()
         for d, peer in enumerate(others, 1):
             over_x(g, i, size, peer, d).start()
-            if i >= direct:
-                @pl.when(lo == 0)
-                def _():
-                    aside(i, size, (peer // 2) * 2 + 1, d).start()
         to_mate(g, i, size, 0).start()
+
+    def lent_x(owner, i, peer, d):
+        return along(owner, i, 1, peer, send_x.at[d - 1], recv_r.at[d - 1, i - shared])
+
+    def lent_back(owner, first, size, d):
+        return along(owner, first, size, mate, send_c.at[d], recv_s.at[d])
+
+    def take_lent(i):
+        from_acq(mate, i, 1, lent_at(i)).wait_recv()
+        for d, peer in enumerate(others, 1):
+            lent_x(mate, i, peer, d).start()
+        lent_back(mate, i, 1, 0).start()
 
     def relay(first, size):
         for d, owner in enumerate(origins, 1):
             over_x(owner, first, size, mate, d).wait_recv()
-            if first < direct:
-                to_mate(owner, first, size, d).start()
-            else:
-                @pl.when(lo == 1)
-                def _():
-                    to_mate(owner, first, size, d).start()
+            cut = min(max(middle - first, 0), size)
+            for at, length in ((first, cut), (first + cut, size - cut)):
+                if length:
+                    to_mate(owner, at, length, d).start()
+
+    def relay_lent(i):
+        for d, owner in enumerate(mates, 1):
+            lent_x(owner, i, mate, d).wait_recv()
+            lent_back(owner, i, 1, d).start()
 
     def arrived(d, h):
-        to_mate([mate, *mates][d], h * middle, middle, d).wait_recv()
+        owner = [mate, *mates][d]
+        if h == 0:
+            to_mate(owner, 0, middle, d).wait_recv()
+            return
+
+        @pl.when(lo == 0)
+        def _():
+            to_mate(owner, middle, total - middle, d).wait_recv()
+
+        @pl.when(lo == 1)
+        def _():
+            to_mate(owner, middle, shared - middle, d).wait_recv()
 
     for c in range(cap):
         gath[g, c] = send[a * cap + c]
     for d, at in targets:
         for c in range(cap):
             to_acq(d, at, c).start()
-    forward(0, cap)
+    for d, peer in enumerate(others, 1):
+        over_x(g, 0, cap, peer, d).start()
+    to_mate(g, 0, cap, 0).start()
 
     depth = n_acq * cap * HZ
     side = depth // 2
@@ -331,11 +374,27 @@
         )
 
     for i, size in received:
-        from_acq(i, size).wait_recv()
-        forward(i, size)
-    out[...] = place_rows(g, 0)
-    out[...] += place_rows(g, 1)
+        take(i, size)
+
+    @pl.when(lo == 1)
+    def _():
+        for i in range(shared, total - cap):
+            take(i, 1)
+        waiting = list(borrowed)
+        for i in range(total - cap, total):
+            for _ in range(max(1, (len(borrowed) - cap) // 2 - cap // 2 + (i == total - cap))):
+                take_lent(waiting.pop(0))
+            take(i, 1)
+        for j in waiting:
+            take_lent(j)
+
     relay(*groups[0])
+
+    @pl.when(lo == 1)
+    def _():
+        relay(*groups[1])
+        relay_lent(borrowed[0])
+
     others_named = named.at[pl.ds(1, n_grp - 1)]
     naming = pltpu.make_async_remote_copy(
         src_ref=others_named, dst_ref=others_named,
@@ -343,22 +402,43 @@
         device_id=(a, mate), device_id_type=MESH,
     )
     naming.wait_recv()
+    out[...] = place_rows(g, 0)
     for owner in origins:
         out[...] += place_rows(owner, 0)
-    for k in range(1, len(groups)):
-        relay(*groups[k])
-        if k == 1:
-            arrived(0, 0)
-            out[...] += place_rows(mate, 0)
+    arrived(0, 0)
+    out[...] += place_rows(mate, 0)
+
+    @pl.when(lo == 0)
+    def _():
+        lent_back(g, shared, total - shared, 0).wait_recv()
+
+    out[...] += place_rows(g, 1)
     arrived(0, 1)
     out[...] += place_rows(mate, 1)
     for d, owner in enumerate(mates, 1):
         arrived(d, 0)
         out[...] += place_rows(owner, 0)
-    for owner in origins:
-        out[...] += place_rows(owner, 1)
+
+    @pl.when(lo == 1)
+    def _():
+        rest = borrowed[1:]
+        for group in groups[2:]:
+            relay(*group)
+            if rest:
+                relay_lent(rest.pop(0))
+        for i in rest:
+            relay_lent(i)
+
     for d, owner in enumerate(mates, 1):
         arrived(d, 1)
+        out[...] += place_rows(owner, 1)
+
+    @pl.when(lo == 0)
+    def _():
+        for d, owner in enumerate(origins, 1):
+            lent_back(owner, shared, total - shared, d).wait_recv()
+
+    for owner in origins:
         out[...] += place_rows(owner, 1)
 
     naming.wait_send()
@@ -367,18 +447,15 @@
         src_ref=left, dst_ref=left, send_sem=send_a.at[0], recv_sem=recv_a.at[0],
         device_id=(flip(a, 1), g), device_id_type=MESH,
     ).wait_send()
-    to_mate(g, 0, total, 0).wait_send()
-    for d in range(1, n_hi):
-        over_x(g, 0, total, mate, d).wait_send()
-        to_mate(g, 0, direct, d).wait_send()
-
-        @pl.when(lo == 0)
-        def _():
-            aside(direct, total - direct, mate, d).wait_send()
-
-        @pl.when(lo == 1)
-        def _():
-            to_mate(g, direct, total - direct, d).wait_send()
+    sent = [send_x.at[d - 1] for d in range(1, n_hi)] + [send_c.at[d] for d in range(n_hi)]
+    for sem in sent:
+        along(g, 0, shared, mate, sem, recv_s.at[0]).wait_send()
+
+    @pl.when(lo == 1)
+    def _():
+        for sem in sent:
+            for _ in range(2):
+                along(g, shared, total - shared, mate, sem, recv_s.at[0]).wait_send()
 
 
 def body(tile_slabs, dest_rank, block_slot, shifts, blend_weight, parent_map):
@@ -415,10 +492,10 @@
             pltpu.VMEM((n_grp, n_acq * cap, HZ, LANES), jnp.float32),
             pltpu.VMEM((n_grp, 2, HZ, depth), jnp.int32),
             dma((6,)), dma((count // PER_LOAD,)),
-            dma((1,)), dma((n_acq // 2 * (1 + cap),)),
+            dma((1,)), dma((n_acq // 2 * (1 + cap) + (n_acq // 4 + n_acq // 8) * cap,)),
             dma((max(1, n_hi - 1),)), dma((max(1, n_hi - 1), pieces.bit_length())),
             dma((n_hi,)), dma((n_hi, 2)),
-            dma((1,)), dma((1,)),
+            dma((1,)), dma((1,)), dma((max(1, n_hi - 1), max(1, (n_acq // 4 + n_acq // 8) * cap))), dma((n_hi,)),
         ],
         compiler_params=pltpu.CompilerParams(
             collective_id=0, has_side_effects=True, vmem_limit_bytes=VMEM_LIMIT * 2**20

time: 23 us -> 22.5 us (0.978)
  Pallas kernels: 22.1 us -> 21.5 us
    pallas_call x1, Pallas kernels: 22.1 us -> 21.5 us  [body(): pl.pallas_call(functools.partial(kernel, n_acq, n_grp, cap), out_shape=pl...]
where the time goes in v4:
time: 22.5 us; the launch traced here: 22.4 us
  Pallas kernels  21.5 us (96%)
  local copies, waits for them, and re-layouts  0.8 us (4%)
    pallas_call x1, Pallas kernels, body(): pl.pallas_call(functools.partial(kernel, n_acq, n_grp, cap), out_shape=pl...  21.5 us
    unnamed x1, local copies, waits for them, and re-layouts  0.8 us

profile of v4, /device:TPU:0, one launch (start us, length us, event | category | flops | bytes accessed | tf_op | source)
XLA Modules:
  0.0 22.4 jit_solution(13893990735852100425)
XLA Ops:
  0.0 21.5 %shard_map.64 = f32[128,1024]{1,0:T(8,128)S(1)} custom-call(f32[8,16,4096]{2,1,0:T(8,128)} %tile_hbm.1, s32[1,256]{1,0:T(1,128)} %bitcast.8, s32[1,256]{1,0:T(1,128)} %bitcast.9, f32[1,256]{1,0:T(1,128)} %bitcast.10, f32[3,256]{1,0:T(4,128)} %bitcast.7, s32[1,16]{1,0:T(1,128)} %bitcast.11), custom_call_target="tpu_custom_call" | custom-call | tf_op jit(solution)/shard_map/pallas_call | solution.py:473
  21.6 0.8 %copy.8 = f32[2,8,8,1024]{3,2,1,0:T(8,128)} copy(f32[2,8,8,1024]{3,2,1,0:T(8,128)S(1)} %bitcast.6) | data formatting | bytes 1048576

commit v5 on v4

--- a/solution.py
+++ b/solution.py
@@ -37,9 +37,9 @@
     sends = side + near + far + farther
     arrivals = [
         [0] + side + far[:half] + near + far[half:] + farther,
-        [0] + sends,
+        [0] + side + near[:half] + far[:half] + near[half:] + far[half:] + farther,
         [0] + far[:half] + side + far[half:] + near + farther,
-        [0] + side + near + farther[:half] + far + farther[half:],
+        [0] + side + near[:half] + far[:half] + near[half:] + far[half:] + farther,
     ]
     return sends, arrivals
 
@@ -89,7 +89,7 @@
     n_acq, n_grp, cap, tile_hbm, dest_hbm, slot_hbm, weight_hbm, shift_hbm, parent_hbm, out,
     named_by, weight, shift, parent, named_rows, weight_row,
     tile, thin, high, low, half, factor, send, gath, named,
-    meta_sem, load_sem, send_a, recv_a, send_x, recv_x, send_c, recv_c, send_p, recv_p, recv_r, recv_s,
+    meta_sem, load_sem, send_a, recv_a, send_x, recv_x, send_c, recv_c, send_p, recv_p, recv_r, recv_s, known,
 ):
     count = tile.shape[0]
     a, g = lax.axis_index("acq"), lax.axis_index("grp")
@@ -99,15 +99,13 @@
     rows = PAIRS * HZ
 
     barrier = pltpu.get_barrier_semaphore()
-    for d in range(1, n_acq):
-        pl.semaphore_signal(barrier, inc=1, device_id=((a + d) % n_acq, g), device_id_type=MESH)
+    unit = max(1, n_acq // 4)
+    straight = list(range(1, unit)) + list(range(unit, n_acq, unit))
+    for d in straight:
+        pl.semaphore_signal(barrier, inc=1, device_id=(flip(a, d), g), device_id_type=MESH)
     for d in range(1, n_grp):
         pl.semaphore_signal(barrier, inc=1, device_id=(a, (g + d) % n_grp), device_id_type=MESH)
     lent = n_acq // 4 + n_acq // 8
-    for d in range(n_acq - lent, n_acq):
-        @pl.when(lo == 1)
-        def _():
-            pl.semaphore_signal(barrier, inc=1, device_id=(flip(a, d), mate), device_id_type=MESH)
 
     dest, slot = named_by.at[0], named_by.at[1]
     metas = [
@@ -210,7 +208,9 @@
         for p in range(PAIRS):
             send[place, :, pl.ds(p * BX, BX)] = scale * value[p * HZ : (p + 1) * HZ]
 
-    pl.semaphore_wait(barrier, n_acq - 1 + n_grp - 1 + lent * (1 - lo))
+    pl.semaphore_wait(barrier, len(straight) + n_grp - 1)
+    for d in range(1, unit):
+        pl.semaphore_signal(known.at[0], inc=1, device_id=(flip(a, d), g), device_id_type=MESH)
 
     targets, order = layout(a, lo, n_acq)
     total = n_acq * cap
@@ -222,11 +222,7 @@
         size = max(1, total - cap - first)
         groups.append((first, size))
         first += size
-    halved = list(range(shared + (total - shared) // 3, total - cap))
-    borrowed = (
-        list(range(shared, shared + (total - shared) // 3, 2)) + halved
-        + list(range(shared + 1, shared + (total - shared) // 3, 2)) + list(range(total - cap, total))
-    )
+    borrowed = list(range(shared, total))
 
     def landed(at, c):
         late = at // (n_acq // 2)
@@ -284,9 +280,14 @@
     def lent_back(owner, first, size, d):
         return along(owner, first, size, mate, send_c.at[d], recv_s.at[d])
 
+    def lent_past(owner, peer, d):
+        return along(owner, total - 1, 1, peer, send_x.at[d - 1], recv_s.at[d])
+
     def take_lent(i):
         from_acq(mate, i, 1, lent_at(i)).wait_recv()
         for d, peer in enumerate(others, 1):
+            if i == total - 1:
+                lent_past(mate, peer - 1, d).start()
             lent_x(mate, i, peer, d).start()
         lent_back(mate, i, 1, 0).start()
 
@@ -301,7 +302,8 @@
     def relay_lent(i):
         for d, owner in enumerate(mates, 1):
             lent_x(owner, i, mate, d).wait_recv()
-            lent_back(owner, i, 1, d).start()
+            if i < total - 1:
+                lent_back(owner, i, 1, d).start()
 
     def arrived(d, h):
         owner = [mate, *mates][d]
@@ -319,7 +321,9 @@
 
     for c in range(cap):
         gath[g, c] = send[a * cap + c]
-    for d, at in targets:
+    sooner = [(d, at) for d, at in targets if d in straight and d < n_acq - lent]
+    later = [pair for pair in targets if pair not in sooner]
+    for d, at in sooner:
         for c in range(cap):
             to_acq(d, at, c).start()
     for d, peer in enumerate(others, 1):
@@ -361,6 +365,21 @@
     for d in range(1, n_grp):
         telling(d, (g + d) % n_grp).start()
 
+    if unit > 1:
+        pl.semaphore_wait(known.at[0], unit - 1)
+
+    @pl.when(lo == 1)
+    def _():
+        pl.semaphore_signal(known.at[1], inc=1, device_id=(a, mate), device_id_type=MESH)
+
+    for d, at in later:
+        if d == n_acq - lent:
+            @pl.when(lo == 0)
+            def _():
+                pl.semaphore_wait(known.at[1], 1)
+        for c in range(cap):
+            to_acq(d, at, c).start()
+
     upright = lax.broadcasted_iota(jnp.int32, (tall, depth), 0) + g * tall
     across_lane = lax.broadcasted_iota(jnp.int32, (tall, depth), 1) % HZ
 
@@ -380,12 +399,15 @@
     def _():
         for i in range(shared, total - cap):
             take(i, 1)
-        waiting = list(borrowed)
-        for i in range(total - cap, total):
-            for _ in range(max(1, (len(borrowed) - cap) // 2 - cap // 2 + (i == total - cap))):
-                take_lent(waiting.pop(0))
+        last = total - cap
+        for i in range(shared, last - cap // 2):
+            take_lent(i)
+        for i in range(last, total):
             take(i, 1)
-        for j in waiting:
+            for j in range(i - cap // 2, i - cap // 2 + 1):
+                if j < last:
+                    take_lent(j)
+        for j in range(last, total):
             take_lent(j)
 
     relay(*groups[0])
@@ -454,8 +476,12 @@
     @pl.when(lo == 1)
     def _():
         for sem in sent:
-            for _ in range(2):
-                along(g, shared, total - shared, mate, sem, recv_s.at[0]).wait_send()
+            along(g, shared, total - shared, mate, sem, recv_s.at[0]).wait_send()
+        lent_back(g, shared, total - shared, 0).wait_send()
+        for d in range(1, n_hi):
+            along(g, shared, total - shared, mate, send_x.at[d - 1], recv_s.at[d]).wait_send()
+            lent_past(g, mate, d).wait_send()
+            lent_back(g, shared, total - 1 - shared, d).wait_send()
 
 
 def body(tile_slabs, dest_rank, block_slot, shifts, blend_weight, parent_map):
@@ -496,6 +522,7 @@
             dma((max(1, n_hi - 1),)), dma((max(1, n_hi - 1), pieces.bit_length())),
             dma((n_hi,)), dma((n_hi, 2)),
             dma((1,)), dma((1,)), dma((max(1, n_hi - 1), max(1, (n_acq // 4 + n_acq // 8) * cap))), dma((n_hi,)),
+            pltpu.SemaphoreType.REGULAR((2,)),
         ],
         compiler_params=pltpu.CompilerParams(
             collective_id=0, has_side_effects=True, vmem_limit_bytes=VMEM_LIMIT * 2**20

time: 22.5 us -> 22.2 us (0.987)
  Pallas kernels: 21.5 us -> 21.2 us
    pallas_call x1, Pallas kernels: 21.5 us -> 21.2 us  [body(): pl.pallas_call(functools.partial(kernel, n_acq, n_grp, cap), out_shape=pl...]
where the time goes in v5:
time: 22.2 us; the launch traced here: 22 us
  Pallas kernels  21.2 us (95%)
  local copies, waits for them, and re-layouts  0.8 us (4%)
    pallas_call x1, Pallas kernels, body(): pl.pallas_call(functools.partial(kernel, n_acq, n_grp, cap), out_shape=pl...  21.2 us
    unnamed x1, local copies, waits for them, and re-layouts  0.8 us

profile of v5, /device:TPU:0, one launch (start us, length us, event | category | flops | bytes accessed | tf_op | source)
XLA Modules:
  0.0 22.0 jit_solution(17069175783406324281)
XLA Ops:
  0.0 21.2 %shard_map.64 = f32[128,1024]{1,0:T(8,128)S(1)} custom-call(f32[8,16,4096]{2,1,0:T(8,128)} %tile_hbm.1, s32[1,256]{1,0:T(1,128)} %bitcast.8, s32[1,256]{1,0:T(1,128)} %bitcast.9, f32[1,256]{1,0:T(1,128)} %bitcast.10, f32[3,256]{1,0:T(4,128)} %bitcast.7, s32[1,16]{1,0:T(1,128)} %bitcast.11), custom_call_target="tpu_custom_call" | custom-call | tf_op jit(solution)/shard_map/pallas_call | solution.py:499
  21.2 0.8 %copy.8 = f32[2,8,8,1024]{3,2,1,0:T(8,128)} copy(f32[2,8,8,1024]{3,2,1,0:T(8,128)S(1)} %bitcast.6) | data formatting | bytes 1048576

commit v6 on v5

--- a/solution.py
+++ b/solution.py
@@ -38,7 +38,7 @@
     arrivals = [
         [0] + side + far[:half] + near + far[half:] + farther,
         [0] + side + near[:half] + far[:half] + near[half:] + far[half:] + farther,
-        [0] + far[:half] + side + far[half:] + near + farther,
+        [0] + far[:half] + side + near[:half] + far[half:] + near[half:] + farther,
         [0] + side + near[:half] + far[:half] + near[half:] + far[half:] + farther,
     ]
     return sends, arrivals

time: 22.2 us -> 21.8 us (0.982)
  Pallas kernels: 21.2 us -> 20.8 us
    pallas_call x1, Pallas kernels: 21.2 us -> 20.8 us  [body(): pl.pallas_call(functools.partial(kernel, n_acq, n_grp, cap), out_shape=pl...]
where the time goes in v6:
time: 21.8 us; the launch traced here: 21.6 us
  Pallas kernels  20.8 us (95%)
  local copies, waits for them, and re-layouts  0.8 us (4%)
    pallas_call x1, Pallas kernels, body(): pl.pallas_call(functools.partial(kernel, n_acq, n_grp, cap), out_shape=pl...  20.8 us
    unnamed x1, local copies, waits for them, and re-layouts  0.8 us

profile of v6, /device:TPU:0, one launch (start us, length us, event | category | flops | bytes accessed | tf_op | source)
XLA Modules:
  0.0 21.6 jit_solution(9945356834800409687)
XLA Ops:
  0.0 20.8 %shard_map.64 = f32[128,1024]{1,0:T(8,128)S(1)} custom-call(f32[8,16,4096]{2,1,0:T(8,128)} %tile_hbm.1, s32[1,256]{1,0:T(1,128)} %bitcast.8, s32[1,256]{1,0:T(1,128)} %bitcast.9, f32[1,256]{1,0:T(1,128)} %bitcast.10, f32[3,256]{1,0:T(4,128)} %bitcast.7, s32[1,16]{1,0:T(1,128)} %bitcast.11), custom_call_target="tpu_custom_call" | custom-call | tf_op jit(solution)/shard_map/pallas_call | solution.py:499
  20.8 0.8 %copy.8 = f32[2,8,8,1024]{3,2,1,0:T(8,128)} copy(f32[2,8,8,1024]{3,2,1,0:T(8,128)S(1)} %bitcast.6) | data formatting | bytes 1048576
